TPU v7x, 128 devices: a whole 4x4x4 slice. The times are simulated.
128 devices in a mesh: row: 8 (over y, core), col: 16 (over z, x).
Axes of the slice: x: 4, y: 4, z: 4, core: 2. Of those that a mesh axis runs over, the one named last changes fastest.
Arguments:
- images: bfloat16 [16384, 768], P(('row', 'col')), may hold values from -5 to 5
- texts: bfloat16 [16384, 768], P(('col', 'row')), may hold values from -5 to 5
- audio: bfloat16 [16384, 768], P(('col', 'row')), may hold values from -5 to 5
Outputs:
- grad_images: float32 [16384, 768], P(('row', 'col'))
- grad_texts: float32 [16384, 768], P(('col', 'row'))
- grad_audio: float32 [16384, 768], P(('col', 'row'))
All inputs are finite; a program needn't handle non-finite values.
Results may differ from a plain program's by a relative error of at most 0.013.
Values may be sent and summed in bfloat16 or wider, within the bound.
A program may use at most 128 MiB of HBM per device.

v0:
```python
import jax
import jax.numpy as jnp
from jax import lax
from jax.sharding import Mesh
from jax.sharding import PartitionSpec as P

ITERS = 3
COL = ("col_0", "col_1")
ROW_COL = ("row", "col_0", "col_1")
COL_ROW = ("col_0", "col_1", "row")


logit_softness = 0.07
target_softness = 0.05
epsilon = 1e-06


def in_one_piece(arrays, axis, dim, along):
    both = jnp.concatenate(arrays, axis=along)
    filled, at, outs = (lax.all_gather(both, axis, axis=dim, tiled=True), 0, [])
    for a in arrays:
        outs.append(lax.slice_in_dim(filled, at, at + a.shape[along], axis=along))
        at += a.shape[along]
    return tuple(outs)


def from_everyone(value, axis):
    size = lax.axis_size(axis)
    return lax.all_to_all(
        jnp.broadcast_to(value[None], (size, *value.shape)), axis, 0, 0, tiled=True
    )


def taken_together(value, axis):
    everything = from_everyone(value, axis)
    return jnp.sum(everything, axis=0)


def in_one(arrays, axis):
    ends = [0]
    for a in arrays:
        ends.append(ends[-1] + a.size)
    subtotal = taken_together(jnp.concatenate([a.ravel() for a in arrays]), axis)
    return tuple((subtotal[b:e].reshape(a.shape) for a, b, e in zip(arrays, ends, ends[1:])))


def summed_rows(terms, axes):
    subtotal = terms.astype(jnp.bfloat16)
    for axis in axes:
        subtotal = lax.psum_scatter(subtotal, axis, scatter_dimension=0, tiled=True)
    return subtotal.astype(jnp.float32)


def cut_along(value, dim, size):
    shape = value.shape
    blocks = value.reshape(*shape[:dim], size, shape[dim] // size, *shape[dim + 1 :])
    return jnp.moveaxis(blocks, dim, 0)


def summed_on_arrival(value, axis, dim):
    blocks = cut_along(value, dim, lax.axis_size(axis))
    arrived = lax.all_to_all(blocks, axis, split_axis=0, concat_axis=0, tiled=True)
    return arrived.astype(jnp.float32).sum(axis=0)


def normalize(raw):
    values = raw.astype(jnp.float32)
    inverse = lax.rsqrt(jnp.sum(values * values, axis=1, keepdims=True) + epsilon)
    return (values * inverse, inverse)


def backward(unit, inverse, incoming):
    return (incoming - unit * jnp.sum(unit * incoming, axis=1, keepdims=True)) * inverse


def shards(images, texts, audio):
    img_unit, img_inverse = normalize(images)
    txt_unit, txt_inverse = normalize(texts)
    aud_unit, aud_inverse = normalize(audio)
    img_rows = lax.all_gather(img_unit.astype(jnp.bfloat16), COL, axis=0, tiled=True)
    text_columns, audio_columns = in_one_piece(
        (txt_unit.astype(jnp.bfloat16), aud_unit.astype(jnp.bfloat16)), "row", 0, 1
    )
    paired_cols = jnp.concatenate([text_columns, audio_columns], axis=0)
    contract = (((1,), (1,)), ((), ()))
    cosine_matrix = lax.dot_general(
        img_rows, paired_cols, contract, preferred_element_type=jnp.float32
    )
    row_extent = img_rows.shape[0]
    column_width = text_columns.shape[0]
    loss_routine = jnp.exp(cosine_matrix / target_softness).reshape(row_extent, 2, column_width)
    softmax_exponent = jnp.exp(cosine_matrix / logit_softness).reshape(row_extent, 2, column_width)
    cols_scale = jnp.ones((2, column_width), jnp.float32)
    opening = 0
    row_sums, row_total = in_one(
        (jnp.sum(loss_routine * cols_scale[None], axis=2), jnp.sum(softmax_exponent, axis=2)), COL
    )
    rows_scale = 1.0 / row_sums
    col_sums, col_total = in_one(
        (jnp.sum(loss_routine * rows_scale[:, :, None], axis=0), jnp.sum(softmax_exponent, axis=0)),
        "row",
    )
    cols_scale = 1.0 / col_sums
    opening = 1
    for iteration in range(opening, ITERS):
        row_sums = taken_together(jnp.sum(loss_routine * cols_scale[None], axis=2), COL)
        rows_scale = 1.0 / row_sums
        col_sums = taken_together(jnp.sum(loss_routine * rows_scale[:, :, None], axis=0), "row")
        cols_scale = 1.0 / col_sums
    target = loss_routine * rows_scale[:, :, None] * cols_scale[None]
    row_mass = taken_together(jnp.sum(target, axis=2), COL)
    score_grad = (
        softmax_exponent / row_total[:, :, None] * row_mass[:, :, None]
        - target
        + softmax_exponent / col_total[None]
        - target
    )
    score_matrix = score_grad.astype(jnp.bfloat16).reshape(row_extent, 2 * column_width)
    owned = images.shape[0]
    image_gradient = summed_rows(
        jnp.dot(score_matrix, paired_cols, preferred_element_type=jnp.float32) / logit_softness, COL
    )
    text_part = lax.slice_in_dim(score_matrix, 0, owned * lax.axis_size("row"), axis=1)
    audio_part = lax.dynamic_slice_in_dim(
        score_matrix, column_width, owned * lax.axis_size("row"), 1
    )
    down = (((0,), (0,)), ((), ()))
    text_gradient_out = lax.dot_general(
        text_part, img_rows, down, preferred_element_type=jnp.float32
    )
    audio_gradient_out = lax.dot_general(
        audio_part, img_rows, down, preferred_element_type=jnp.float32
    )
    paired_grad = summed_on_arrival(
        (jnp.concatenate([text_gradient_out, audio_gradient_out], axis=1) / logit_softness).astype(
            jnp.bfloat16
        ),
        "row",
        0,
    )
    width = images.shape[1]
    grad_txt = backward(txt_unit, txt_inverse, paired_grad[:, :width])
    grad_aud = backward(aud_unit, aud_inverse, paired_grad[:, width:])
    return (backward(img_unit, img_inverse, image_gradient), grad_txt, grad_aud)


def solution(mesh):
    split = Mesh(mesh.devices.reshape(mesh.shape["row"], 4, 4), ("row", "col_0", "col_1"))
    placed = (P(ROW_COL, None), P(COL_ROW, None), P(COL_ROW, None))
    return jax.shard_map(
        shards,
        mesh=split,
        in_specs=placed,
        out_specs=(P(ROW_COL, None), P(COL_ROW, None), P(COL_ROW, None)),
        check_vma=False,
    )
```

profile of v0, /device:TPU:0, one launch (start us, length us, event | category | flops | bytes accessed | tf_op | source)
XLA Modules:
  0.0 329.2 jit_solution(17503242842045232137)
XLA Ops:
  9.3 1.2 fusion.20
  12.4 1.7 fusion.25
  14.1 27.5 %all-gather.5.cloned.1.call-done = bf16[1024,1536]{1,0:T(8,128)(2,1)} async-done(((bf16[128,1536]{1,0:T(8,128)(2,1)}), bf16[1024,1536]{1,0:T(8,128)(2,1)}) %all-gather.5.cloned.1.call-update) | async-done | bytes 3145744 | tf_op jit(solution)/shard_map/all_gather | solution.py:20
  41.6 3.2 fusion.39
  44.9 47.4 %all-gather.3.cloned.1.call-done = bf16[2048,768]{1,0:T(8,128)(2,1)} async-done(((bf16[128,768]{1,0:T(8,128)(2,1)}), bf16[2048,768]{1,0:T(8,128)(2,1)}) %all-gather.3.cloned.1.call-update) | async-done | bytes 3145744 | tf_op jit(solution)/shard_map/all_gather | solution.py:80
  92.2 14.3 %bitcast_reduce_fusion.1 = (f32[2048,2]{0,1:T(2,128)S(1)}, f32[2048,2]{0,1:T(2,128)S(1)}, f32[2048,2048]{0,1:T(8,128)}) fusion(bf16[2048,768]{1,0:T(8,128)(2,1)} %all-gather.3.cloned.1.call-done, bf16[1024,768]{1,0:T(8,128)(2,1)} %get-tuple-element.10, bf16[1024,768]{1,0:T(8,128)(2,1)S(1)} %get-tuple-element.9), kind=kOutput, calls=%fused_computation.15 | convolution fusion | flops 6465511424 | bytes 23101440 | tf_op jit(solution)/shard_map/dot_general | solution.py:86
  108.6 15.1 %all_to_all.42 = f32[16,1,8192]{2,1,0:T(1,128)S(1)} all-to-all(f32[16,1,8192]{2,1,0:T(1,128)S(1)} %broadcast_in_dim.18), channel_id=1, replica_groups=mesh['row'=8,'col_0'=4,'col_1'=4] {'col_0','col_1'}, dimensions={0} | all-to-all | bytes 1048576 | tf_op jit(solution)/shard_map/all_to_all | solution.py:29
  125.4 8.5 %fusion.5 = (f32[2048]{0:T(1024)S(1)}, f32[2048]{0:T(1024)S(1)}) fusion(f32[2048,2]{0,1:T(2,128)S(1)} %copy.20, f32[2048,2048]{0,1:T(8,128)} %get-tuple-element.17), kind=kLoop, calls=%fused_computation.9 | loop fusion | flops 20967424 | bytes 16809984 | tf_op jit(solution)/shard_map/reduce_sum | solution.py:100
  134.0 10.2 %all_to_all.43 = f32[8,1,4096]{2,1,0:T(1,128)S(1)} all-to-all(f32[8,1,4096]{2,1,0:T(1,128)S(1)} %broadcast_in_dim.19), channel_id=1, replica_groups=mesh['row'=8,'col_0'=4,'col_1'=4] {'row'}, dimensions={0} | all-to-all | bytes 262144 | tf_op jit(solution)/shard_map/all_to_all | solution.py:29
  144.3 7.4 %fusion.6 = f32[2048,2]{0,1:T(2,128)S(1)} fusion(f32[2,1024]{1,0:T(2,128)S(1)} %div.98, f32[2048,2048]{0,1:T(8,128)} %get-tuple-element.17), kind=kLoop, calls=%fused_computation.16 | loop fusion | flops 12578816 | bytes 16801792 | tf_op jit(solution)/shard_map/reduce_sum | solution.py:106
  151.8 11.6 %all_to_all.44 = f32[16,2048,2]{1,2,0:T(2,128)S(1)} all-to-all(f32[16,2048,2]{1,2,0:T(2,128)S(1)} %broadcast_in_dim.20), channel_id=1, replica_groups=mesh['row'=8,'col_0'=4,'col_1'=4] {'col_0','col_1'}, dimensions={0} | all-to-all | bytes 524288 | tf_op jit(solution)/shard_map/all_to_all | solution.py:29
  163.5 8.6 %fusion.4 = f32[2048]{0:T(1024)S(1)} fusion(f32[2048,2]{0,1:T(2,128)S(1)} %broadcast_divide_fusion.1, f32[2048,2048]{0,1:T(8,128)} %get-tuple-element.17), kind=kLoop, calls=%fused_computation.7 | loop fusion | flops 12580864 | bytes 16801792 | tf_op jit(solution)/shard_map/reduce_sum | solution.py:108
  172.2 8.0 %all_to_all.45 = f32[8,2,1024]{2,1,0:T(2,128)S(1)} all-to-all(f32[8,2,1024]{2,1,0:T(2,128)S(1)} %broadcast_in_dim.22), channel_id=1, replica_groups=mesh['row'=8,'col_0'=4,'col_1'=4] {'row'}, dimensions={0} | all-to-all | bytes 131072 | tf_op jit(solution)/shard_map/all_to_all | solution.py:29
  180.2 7.4 %fusion.7 = f32[2048,2]{0,1:T(2,128)S(1)} fusion(f32[2,1024]{1,0:T(2,128)S(1)} %broadcast_divide_fusion.3, f32[2048,2048]{0,1:T(8,128)} %get-tuple-element.17), kind=kLoop, calls=%fused_computation.17 | loop fusion | flops 12578816 | bytes 16801792 | tf_op jit(solution)/shard_map/reduce_sum | solution.py:106
  187.7 11.6 %all_to_all.46 = f32[16,2048,2]{1,2,0:T(2,128)S(1)} all-to-all(f32[16,2048,2]{1,2,0:T(2,128)S(1)} %broadcast_in_dim.23), channel_id=1, replica_groups=mesh['row'=8,'col_0'=4,'col_1'=4] {'col_0','col_1'}, dimensions={0} | all-to-all | bytes 524288 | tf_op jit(solution)/shard_map/all_to_all | solution.py:29
  199.4 8.6 %fusion.10 = f32[2048]{0:T(1024)S(1)} fusion(f32[2048,2]{0,1:T(2,128)S(1)} %broadcast_divide_fusion, f32[2048,2048]{0,1:T(8,128)} %get-tuple-element.17), kind=kLoop, calls=%fused_computation.22 | loop fusion | flops 12580864 | bytes 16801792 | tf_op jit(solution)/shard_map/reduce_sum | solution.py:108
  208.0 8.0 %all_to_all.47 = f32[8,2,1024]{2,1,0:T(2,128)S(1)} all-to-all(f32[8,2,1024]{2,1,0:T(2,128)S(1)} %broadcast_in_dim.25), channel_id=1, replica_groups=mesh['row'=8,'col_0'=4,'col_1'=4] {'row'}, dimensions={0} | all-to-all | bytes 131072 | tf_op jit(solution)/shard_map/all_to_all | solution.py:29
  216.0 7.6 %fusion.9 = f32[2048,2]{0,1:T(2,128)S(1)} fusion(f32[2,1024]{1,0:T(2,128)S(1)} %broadcast_divide_fusion.2, f32[2048,2]{0,1:T(2,128)S(1)} %broadcast_divide_fusion, f32[2048,2048]{0,1:T(8,128)} %get-tuple-element.17), kind=kLoop, calls=%fused_computation.19 | loop fusion | flops 16773120 | bytes 16818176 | tf_op jit(solution)/shard_map/reduce_sum | solution.py:111
  224.5 3.5 %all-to-all-start.6 = ((f32[16,2048,2]{1,2,0:T(2,128)}), f32[16,2048,2]{1,2,0:T(2,128)S(1)}, u32[]{:S(2)}, u32[]{:S(2)}) async-start(f32[16,2048,2]{1,2,0:T(2,128)} %broadcast_in_dim.26), calls=%async_computation.6 | async-start | bytes 524288 | tf_op jit(solution)/shard_map/all_to_all | solution.py:29
  229.6 7.2 %all-to-all-done.6 = f32[16,2048,2]{1,2,0:T(2,128)S(1)} async-done(((f32[16,2048,2]{1,2,0:T(2,128)}), f32[16,2048,2]{1,2,0:T(2,128)S(1)}, u32[]{:S(2)}, u32[]{:S(2)}) %all-to-all-start.6) | async-done | bytes 262176 | tf_op jit(solution)/shard_map/all_to_all | solution.py:29
  236.9 12.1 %fusion.3 = bf16[2048,2048]{0,1:T(8,128)(2,1)S(1)} fusion(f32[2048,2048]{0,1:T(8,128)} %get-tuple-element.17, f32[2048]{0:T(1024)S(1)} %get-tuple-element.16, f32[2048]{0:T(1024)S(1)} %bitcast.56, f32[2048,2]{0,1:T(2,128)S(1)} %reduce_sum.225, f32[2048,2]{0,1:T(2,128)S(1)} %broadcast_divide_fusion, f32[2048,2]{0,1:T(2,128)S(1)} %copy.19), kind=kLoop, calls=%fused_computation.4 | loop fusion | flops 46137344 | bytes 25231360 | tf_op jit(solution)/shard_map/convert_element_type | solution.py:118
  249.0 3.2 copy-done
  252.2 8.5 %multiply_convert_fusion = bf16[2048,768]{1,0:T(8,128)(2,1)} fusion(bf16[2048,2048]{0,1:T(8,128)(2,1)S(1)} %fusion.3, bf16[1024,768]{1,0:T(8,128)(2,1)S(1)} %copy-done.4, bf16[1024,768]{1,0:T(8,128)(2,1)S(1)} %get-tuple-element.9), kind=kOutput, calls=%fused_computation.27 | convolution fusion | flops 6451888128 | bytes 14680064 | tf_op jit(solution)/shard_map/dot_general | solution.py:121
  260.8 6.3 %fusion.13 = f32[1024,768]{1,0:T(8,128)S(1)} fusion(bf16[2048,768]{1,0:T(8,128)(2,1)} %all-gather.3.cloned.1.call-done, bf16[2048,2048]{0,1:T(8,128)(2,1)} %copy-done), kind=kOutput, calls=%fused_computation.28 | convolution fusion | flops 3221225472 | bytes 10485760 | tf_op jit(solution)/shard_map/dot_general | solution.py:131
  267.9 3.4 %fusion.15 = f32[1024,768]{1,0:T(8,128)S(1)} fusion(bf16[2048,768]{1,0:T(8,128)(2,1)S(1)} %copy-done.5, bf16[2048,2048]{0,1:T(8,128)(2,1)S(1)} %copy-done.1), kind=kOutput, calls=%fused_computation.30 | convolution fusion | flops 3221225472 | bytes 10485760 | tf_op jit(solution)/shard_map/dot_general | solution.py:128
  271.3 2.3 fusion.12
  273.6 3.6 %all-to-all-start.7 = ((bf16[8,128,1536]{2,1,0:T(8,128)(2,1)}), bf16[8,128,1536]{2,1,0:T(8,128)(2,1)S(1)}, u32[]{:S(2)}, u32[]{:S(2)}) async-start(bf16[8,128,1536]{2,1,0:T(8,128)(2,1)} %fusion.12), calls=%async_computation.9 | async-start | bytes 6291456 | tf_op jit(solution)/shard_map/all_to_all | solution.py:62
  277.4 17.7 %reduce-scatter.3.cloned.1.call-done = bf16[512,768]{1,0:T(8,128)(2,1)} async-done(((bf16[2048,768]{1,0:T(8,128)(2,1)}), bf16[512,768]{1,0:T(8,128)(2,1)}) %reduce-scatter.3.cloned.1.call-update) | async-done | bytes 786448 | tf_op jit(solution)/shard_map/reduce_scatter | solution.py:50
  295.1 20.6 %all-to-all-done.7 = bf16[8,128,1536]{2,1,0:T(8,128)(2,1)S(1)} async-done(((bf16[8,128,1536]{2,1,0:T(8,128)(2,1)}), bf16[8,128,1536]{2,1,0:T(8,128)(2,1)S(1)}, u32[]{:S(2)}, u32[]{:S(2)}) %all-to-all-start.7) | async-done | bytes 3145760 | tf_op jit(solution)/shard_map/all_to_all | solution.py:62
  317.4 2.0 reduce-scatter.5.cloned.1.call-done
  319.4 1.2 fusion.35
  320.6 2.0 fusion.36
  (64 shorter events, 13.7 us)
Async XLA Ops:
  7.2 34.5 %all-gather.5.cloned.1.call-start = ((), (), s32[]{:S(2)}) async-start(), calls=%async_computation.11 | async-start | bytes 3538944 | tf_op jit(solution)/shard_map/all_gather | solution.py:20
  11.3 80.9 %all-gather.3.cloned.1.call-start = ((), (), s32[]{:S(2)}) async-start(), calls=%async_computation.10 | async-start | bytes 3342336 | tf_op jit(solution)/shard_map/all_gather | solution.py:80
  224.5 12.4 %all-to-all-start.6 = ((f32[16,2048,2]{1,2,0:T(2,128)}), f32[16,2048,2]{1,2,0:T(2,128)S(1)}, u32[]{:S(2)}, u32[]{:S(2)}) async-start(f32[16,2048,2]{1,2,0:T(2,128)} %broadcast_in_dim.26), calls=%async_computation.6 | async-start | bytes 524288 | tf_op jit(solution)/shard_map/all_to_all | solution.py:29
  228.0 67.1 %reduce-scatter.3.cloned.1.call-start = ((), (), s32[]{:S(2)}) async-start(), calls=%async_computation.12 | async-start | bytes 3932160 | tf_op jit(solution)/shard_map/reduce_scatter | solution.py:50
  236.9 15.3 %copy-start.4 = (bf16[1024,768]{1,0:T(8,128)(2,1)S(1)}, bf16[1024,768]{1,0:T(8,128)(2,1)}, u32[]{:S(2)}) copy-start(bf16[1024,768]{1,0:T(8,128)(2,1)} %get-tuple-element.10) | copy-start | bytes 4718596
  249.0 3.2 copy-start
  260.8 6.3 %copy-start.1 = (bf16[2048,2048]{0,1:T(8,128)(2,1)S(1)}, bf16[2048,2048]{0,1:T(8,128)(2,1)}, u32[]{:S(2)}) copy-start(bf16[2048,2048]{0,1:T(8,128)(2,1)} %copy-done) | copy-start | bytes 25165828
  260.8 7.0 %copy-start.5 = (bf16[2048,768]{1,0:T(8,128)(2,1)S(1)}, bf16[2048,768]{1,0:T(8,128)(2,1)}, u32[]{:S(2)}) copy-start(bf16[2048,768]{1,0:T(8,128)(2,1)} %all-gather.3.cloned.1.call-done) | copy-start | bytes 9437188
  271.3 44.8 %copy-start.2 = (bf16[128,768]{1,0:T(8,128)(2,1)S(1)}, bf16[128,768]{1,0:T(8,128)(2,1)}, u32[]{:S(2)}) copy-start(bf16[128,768]{1,0:T(8,128)(2,1)} %param.5) | copy-start | bytes 589828
  271.3 44.8 %copy-start.3 = (bf16[128,768]{1,0:T(8,128)(2,1)S(1)}, bf16[128,768]{1,0:T(8,128)(2,1)}, u32[]{:S(2)}) copy-start(bf16[128,768]{1,0:T(8,128)(2,1)} %param.4) | copy-start | bytes 589828
  273.6 42.0 %all-to-all-start.7 = ((bf16[8,128,1536]{2,1,0:T(8,128)(2,1)}), bf16[8,128,1536]{2,1,0:T(8,128)(2,1)S(1)}, u32[]{:S(2)}, u32[]{:S(2)}) async-start(bf16[8,128,1536]{2,1,0:T(8,128)(2,1)} %fusion.12), calls=%async_computation.9 | async-start | bytes 6291456 | tf_op jit(solution)/shard_map/all_to_all | solution.py:62
  277.3 42.1 %reduce-scatter.5.cloned.1.call-start = ((), (), s32[]{:S(2)}) async-start(), calls=%async_computation.13 | async-start | bytes 983040 | tf_op jit(solution)/shard_map/reduce_scatter | solution.py:50
Sparse Core Ops, SparseCore 0:
  11.4 30.1 all-gather.4
  44.3 47.8 all-gather.2
  260.9 34.0 reduce-scatter.2
  297.3 22.0 reduce-scatter.4
where the time goes:
time: 330 us; the launch traced here: 329 us
  waiting for transfers between devices  122 us (37%)
  other arithmetic  75.1 us (23%)
  blocking collectives  64.5 us (20%)
  matrix products  32.5 us (10%)
  between operations  14.1 us (4%)
  local copies, waits for them, and re-layouts  13.1 us (4%)
  starting transfers between devices  7.57 us (2%)
    all_to_all x6, blocking collectives, from_everyone(): lax.all_to_all(jnp.broadcast_to(value[None], (size, *value.shape)), axis,...  64.5 us
    all_gather x1, waiting for transfers between devices, shards(): lax.all_gather(img_unit.astype(jnp.bfloat16), COL, axis=0, tiled=True)  47.4 us
    all_gather x1, waiting for transfers between devices, in_one_piece(): filled, at, outs = (lax.all_gather(both, axis, axis=dim, tiled=True), 0, [])  27.5 us
    reduce_sum x3, other arithmetic, shards(): jnp.sum(loss_routine * rows_scale[:, :, None], axis=0)  25.7 us
    all_to_all x1, waiting for transfers between devices, summed_on_arrival(): lax.all_to_all(blocks, axis, split_axis=0, concat_axis=0, tiled=True)  20.6 us
    reduce_scatter x2, waiting for transfers between devices, summed_rows(): subtotal = lax.psum_scatter(subtotal, axis, scatter_dimension=0, tiled=True)  19.7 us
    reduce_sum x2, other arithmetic, shards(): jnp.sum(loss_routine * cols_scale[None], axis=2)  14.7 us
    dot_general x1, matrix products, shards(): lax.dot_general(img_rows, paired_cols, contract, preferred_element_type=j...  14.3 us
  transfers between devices with their start and end apart: 6, of which 6 were waited for; matrix products, arithmetic and copies ran while one was open for 6% of the time, Pallas kernels for 0%

commit v1 on v0

v1 whole, which is shorter than its diff:
```python
import functools

import jax
import jax.numpy as jnp
from jax import lax
from jax.experimental import pallas as pl
from jax.experimental.pallas import tpu as pltpu
from jax.sharding import PartitionSpec as P

ITERS = 3
logit_softness = 0.07
target_softness = 0.05
epsilon = 1e-06
LOG2E = 1.4426950408889634

MESH = pl.DeviceIdType.MESH
F32 = jnp.float32
BF16 = jnp.bfloat16
B = 128
D = 768
POS = [(2, 2), (1, 2), (3, 2), (0, 2), (2, 1), (2, 3), (2, 0), (1, 1), (1, 3), (3, 1), (3, 3), (0, 1), (0, 3), (1, 0), (3, 0), (0, 0)]
PI = {p: i for i, p in enumerate(POS)}
COLS = [(2, 0), (2, 1), (1, 0), (1, 1), (3, 0), (3, 1), (0, 0), (0, 1)]
CI = {p: i for i, p in enumerate(COLS)}
NSEM = 144


class Net:
    def __init__(self, send_sem, recv_sem):
        self.send_sem, self.recv_sem = send_sem, recv_sem
        self.index, self.sent = {}, []

    def at(self, tag):
        return self.index.setdefault(tag, len(self.index))

    def copy(self, tag, src, dst, device):
        i = self.at(tag)
        return pltpu.make_async_remote_copy(
            src_ref=src, dst_ref=dst, send_sem=self.send_sem.at[i], recv_sem=self.recv_sem.at[i],
            device_id=device, device_id_type=MESH,
        )

    def send(self, tag, src, dst, device):
        self.sent.append((tag, src, dst, device))
        self.make(tag, src, dst, device).start()

    def make(self, tag, src, dst, device):
        return self.copy(tag, src() if callable(src) else src, dst() if callable(dst) else dst, device)

    def wait(self, tag, landed, device):
        self.copy(tag, landed, landed, device).wait_recv()

    def drain(self):
        for entry in self.sent:
            self.make(*entry).wait_send()


def unit_of(raw_ref):
    values = raw_ref[...].astype(F32)
    inverse = lax.rsqrt(jnp.sum(values * values, axis=1, keepdims=True) + epsilon)
    return values * inverse, inverse


def lanes_to_rows(row):
    return jnp.broadcast_to(row, (B, B)).T


def kernel(
    img_in, txt_in, aud_in, out_img, out_txt, out_aud,
    img, cols, K, E, S,
    rows_local, rows_sent, rows_got, cols_local, cols_sent, cols_got, avec, bvec, rho, ict,
    st1, r1, st2, r2, st3, r3, st4, r4,
    gsib, sibgot, yst1, yr1, yst2, yr2,
    net_send, net_recv, rsend, rrecv, csend, crecv,
):
    row, col = lax.axis_index("row"), lax.axis_index("col")
    y, core = row // 2, lax.rem(row, 2)
    z, x = col // 4, lax.rem(col, 4)

    def wrap(v):
        return lax.rem(v, 4)

    def zx(dz, dx):
        return wrap(z + dz) * 4 + wrap(x + dx)

    def yc(dy, own):
        return wrap(y + dy) * 2 + (core if own else 1 - core)

    col_of = [zx(dz, dx) for dz, dx in POS]
    row_of = [yc(dy, own) for dy, own in COLS]

    def at_zx(dz, dx):
        return (row, col_of[PI[dz % 4, dx % 4]])

    def at_y(dy, own=1):
        return (row_of[CI[dy % 4, own]], col)

    barrier = pltpu.get_barrier_semaphore()
    for i in range(15):
        pl.semaphore_signal(barrier, inc=1, device_id=(row, col_of[i]), device_id_type=MESH)
    for i in range(7):
        pl.semaphore_signal(barrier, inc=1, device_id=(row_of[i], col), device_id_type=MESH)

    def image(dz, dx, start=0, count=B):
        return img.at[pl.ds(PI[dz % 4, dx % 4] * B + start, count), :]

    def column(m, dy, own, start=0, count=B):
        return cols.at[m, pl.ds(CI[dy % 4, own] * B + start, count), :]

    image(0, 0)[...] = unit_of(img_in)[0].astype(BF16)
    column(0, 0, 1)[...] = unit_of(txt_in)[0].astype(BF16)
    column(1, 0, 1)[...] = unit_of(aud_in)[0].astype(BF16)
    pl.semaphore_wait(barrier, 22)

    net = Net(net_send, net_recv)

    def place(h, first, second):
        return (first, second) if h == 0 else (second, first)

    def half_dev(h, first, second):
        return at_zx(*place(h, first, second))

    def first_send(h):
        for step in (1, 3):
            net.send(("g1", h, step), image(0, 0, 64 * h, 64), image(*place(h, -step, 0), 64 * h, 64), half_dev(h, step, 0))

    def second_send(h, f):
        for step in (1, 3):
            net.send(("g2", h, f, step), image(*place(h, f, 0), 64 * h, 64), image(*place(h, f, -step), 64 * h, 64), half_dev(h, 0, step))

    def first_forward(h, step):
        net.wait(("g1", h, step), image(*place(h, -step, 0), 64 * h, 64), half_dev(h, -step, 0))
        at = 64 * h + (0 if step == 1 else 32)
        net.send(("g1f", h, step), image(*place(h, -step, 0), at, 32), image(*place(h, 2, 0), at, 32), half_dev(h, step, 0))

    def first_end(h):
        for step in (1, 3):
            at = 64 * h + (0 if step == 1 else 32)
            net.wait(("g1f", h, step), image(*place(h, 2, 0), at, 32), half_dev(h, -step, 0))

    def second_forward(h, f):
        for step in (1, 3):
            net.wait(("g2", h, f, step), image(*place(h, f, -step), 64 * h, 64), half_dev(h, 0, -step))
            at = 64 * h + (0 if step == 1 else 32)
            net.send(("g2f", h, f, step), image(*place(h, f, -step), at, 32), image(*place(h, f, 2), at, 32), half_dev(h, 0, step))

    def second_end(h, f):
        for step in (1, 3):
            at = 64 * h + (0 if step == 1 else 32)
            net.wait(("g2f", h, f, step), image(*place(h, f, 2), at, 32), half_dev(h, 0, -step))

    def col_send(m):
        for step in (1, 3):
            net.send(("c1", m, step), column(m, 0, 1), column(m, -step, 1), at_y(step))
        net.send(("cs", m, 0), column(m, 0, 1), column(m, 0, 0), at_y(0, 0))

    def col_forward(m):
        for step in (1, 3):
            net.wait(("c1", m, step), column(m, -step, 1), at_y(-step))
            at = 0 if step == 1 else 64
            net.send(("c1f", m, step), column(m, -step, 1, at, 64), column(m, 2, 1, at, 64), at_y(step))
            net.send(("cs", m, -step % 4), column(m, -step, 1), column(m, -step, 0), at_y(0, 0))

    def col_end(m):
        for step in (1, 3):
            at = 0 if step == 1 else 64
            net.wait(("c1f", m, step), column(m, 2, 1, at, 64), at_y(-step))
        net.send(("cs", m, 2), column(m, 2, 1), column(m, 2, 0), at_y(0, 0))

    def col_rest(m):
        for dy in range(4):
            net.wait(("cs", m, dy), column(m, dy, 0), at_y(0, 0))

    for h in (0, 1):
        first_send(h)
    col_send(0)
    for h in (0, 1):
        second_send(h, 0)
    col_send(1)
    for step in (1, 3):
        for h in (0, 1):
            first_forward(h, step)
    for f in (3, 1):
        for h in (0, 1):
            second_send(h, f)
    col_forward(0)
    for h in (0, 1):
        second_forward(h, 0)
    for h in (0, 1):
        first_end(h)
        second_send(h, 2)
    for h in (0, 1):
        second_forward(h, 3)
    col_forward(1)
    col_end(0)
    for h in (0, 1):
        second_forward(h, 1)
    col_end(1)
    for h in (0, 1):
        second_forward(h, 2)
    for m in (0, 1):
        col_rest(m)
    for f in (0, 3, 1, 2):
        for h in (0, 1):
            second_end(h, f)

    def rows_send(k, m):
        for i in range(16):
            rows_sent[k, m, pl.ds(col_of[i], 1), :] = rows_local[m, i : i + 1, :]
        for i in range(15):
            pltpu.make_async_remote_copy(
                src_ref=rows_sent.at[k, m], dst_ref=rows_got.at[k, m, i], send_sem=rsend.at[k, m], recv_sem=rrecv.at[k, m],
                device_id=(row, col_of[i]), device_id_type=MESH,
            ).start()

    def rows_whole(k, m):
        return pltpu.make_async_remote_copy(
            src_ref=rows_got.at[k, m], dst_ref=rows_got.at[k, m], send_sem=rsend.at[k, m], recv_sem=rrecv.at[k, m],
            device_id=(row, col_of[0]), device_id_type=MESH,
        )

    def rows_sum(k, m):
        rows_whole(k, m).wait_recv()
        return rows_sent[k, m] + jnp.sum(rows_got[k, m], axis=0)

    def cols_send(k, m):
        for i in range(8):
            cols_sent[k, m, pl.ds(row_of[i], 1), :] = cols_local[m, i : i + 1, :]
        for i in range(7):
            pltpu.make_async_remote_copy(
                src_ref=cols_sent.at[k, m], dst_ref=cols_got.at[k, m, i], send_sem=csend.at[k, m], recv_sem=crecv.at[k, m],
                device_id=(row_of[i], col), device_id_type=MESH,
            ).start()

    def cols_whole(k, m):
        return pltpu.make_async_remote_copy(
            src_ref=cols_got.at[k, m], dst_ref=cols_got.at[k, m], send_sem=csend.at[k, m], recv_sem=crecv.at[k, m],
            device_id=(row_of[0], col), device_id_type=MESH,
        )

    def cols_sum(k, m):
        cols_whole(k, m).wait_recv()
        return cols_sent[k, m] + jnp.sum(cols_got[k, m], axis=0)

    def rows_back(dst, m, value):
        rows_local[m] = value
        for i in range(16):
            dst[m, i : i + 1, :] = rows_local[m, pl.ds(col_of[i], 1), :]

    def cols_back(dst, m, value):
        cols_local[m] = value
        for i in range(8):
            dst[m, i : i + 1, :] = cols_local[m, pl.ds(row_of[i], 1), :]

    def tile(j):
        return slice(j * B, (j + 1) * B)

    def row_part(part):
        return jnp.sum(part.T, axis=0, keepdims=True)

    def block(i):
        return pl.ds(pl.multiple_of(i * B, B), B)

    contract = (((1,), (1,)), ((), ()))

    def similarity(m):
        def body(i, carry):
            at = pl.ds(pl.multiple_of(i * 256, 256), 256)
            cosine = lax.dot_general(img[at, :], cols[m], contract, preferred_element_type=F32)
            E[m, at, :] = cosine
            part = jnp.zeros((256, B), F32)
            for j in range(8):
                kern = jnp.exp2(cosine[:, tile(j)] * (LOG2E / target_softness))
                K[m, at, tile(j)] = kern
                part = part + kern
            rows_local[m, pl.ds(2 * i, 1), :] = row_part(part[:B])
            rows_local[m, pl.ds(2 * i + 1, 1), :] = row_part(part[B:])
            return carry

        lax.fori_loop(0, 8, body, 0)

    def fold(value):
        return jnp.sum(value.reshape(16, 8, B), axis=0)

    def close_columns(m, acc):
        for j in range(8):
            cols_local[m, j : j + 1, :] = jnp.sum(acc[j], axis=0, keepdims=True)

    def softmax(m):
        def body(i, acc):
            part = jnp.zeros((B, B), F32)
            out = []
            for j in range(8):
                e = jnp.exp2(E[m, block(i), tile(j)] * (LOG2E / logit_softness))
                E[m, block(i), tile(j)] = e
                part = part + e
                out.append(acc[j] + fold(e))
            rows_local[m, pl.ds(i, 1), :] = row_part(part)
            return tuple(out)

        acc = lax.fori_loop(0, 16, body, tuple(jnp.zeros((8, B), F32) for _ in range(8)))
        close_columns(m, acc)

    def column_pass(m):
        def body(i, acc):
            a = lanes_to_rows(avec[m, pl.ds(i, 1), :])
            return tuple(acc[j] + fold(K[m, block(i), tile(j)] * a) for j in range(8))

        acc = lax.fori_loop(0, 16, body, tuple(jnp.zeros((8, B), F32) for _ in range(8)))
        close_columns(m, acc)

    def row_pass(m):
        def body(i, carry):
            part = K[m, block(i), tile(0)] * bvec[m, 0:1, :]
            for j in range(1, 8):
                part = part + K[m, block(i), tile(j)] * bvec[m, j : j + 1, :]
            rows_local[m, pl.ds(i, 1), :] = row_part(part)
            return carry

        lax.fori_loop(0, 16, body, 0)

    both = (0, 1)
    for m in both:
        similarity(m)
        rows_send(0, m)
    for m in both:
        softmax(m)
        rows_send(ITERS + 1, m)
        cols_send(ITERS, m)
    for sweep in range(ITERS):
        for m in both:
            rows_back(avec, m, 1.0 / rows_sum(sweep, m))
            column_pass(m)
            cols_send(sweep, m)
        for m in both:
            cols_back(bvec, m, 1.0 / cols_sum(sweep, m))
            row_pass(m)
            rows_send(sweep + 1, m)
    for m in both:
        cols_back(ict, m, 1.0 / cols_sum(ITERS, m))
    for m in both:
        rows_back(rho, m, rows_sum(ITERS, m) / rows_sum(ITERS + 1, m))

    for m in both:
        def score(i, carry, m=m):
            a = lanes_to_rows(avec[m, pl.ds(i, 1), :])
            mass = lanes_to_rows(avec[m, pl.ds(i, 1), :] * rho[m, pl.ds(i, 1), :])
            twice = a + a
            for j in range(8):
                soft = E[m, block(i), tile(j)] * (mass + ict[m, j : j + 1, :])
                target = K[m, block(i), tile(j)] * twice * bvec[m, j : j + 1, :]
                S[block(i), m * 1024 + j * B : m * 1024 + (j + 1) * B] = (soft - target).astype(BF16)
            return carry

        lax.fori_loop(0, 16, score, 0)

    def part_of(h, first, second, start=0, count=64):
        dz, dx = place(h, first % 4, second % 4)
        at = PI[dz, dx] * B + 64 * h + start
        return K[0, at : at + count, 0:D]

    def near_dev(h, step):
        return half_dev(h, 0, step)

    def far_dev(h, step):
        return half_dev(h, step, 0)

    def reduce1(h, f):
        st1[h, f] = part_of(h, f, 2).astype(BF16)
        for s, step in enumerate((1, 3)):
            net.send(
                ("r1", h, f, s), lambda s=s: st1.at[h, f, pl.ds(32 * s, 32), :], lambda s=s: r1.at[h, f, s], near_dev(h, step)
            )

    def reduce2(h, f, s):
        step = (1, 3)[s]
        net.wait(("r1", h, f, s), r1.at[h, f, s], near_dev(h, -step))
        for t in (0, 1):
            value = part_of(h, f, step, 32 * t, 32)
            if s == t:
                value = value + r1[h, f, s].astype(F32)
            st2[h, f, s, 32 * t : 32 * t + 32, :] = value.astype(BF16)
        net.send(("r2", h, f, s), lambda: st2.at[h, f, s], lambda: r2.at[h, f, s], near_dev(h, step))

    def line(h, f):
        for s, step in enumerate((1, 3)):
            net.wait(("r2", h, f, s), r2.at[h, f, s], near_dev(h, -step))
        return part_of(h, f, 0) + r2[h, f, 0].astype(F32) + r2[h, f, 1].astype(F32)

    def reduce3(h):
        st3[h] = line(h, 2).astype(BF16)
        for s, step in enumerate((1, 3)):
            net.send(("r3", h, s), st3.at[h, pl.ds(32 * s, 32), :], r3.at[h, s], far_dev(h, step))

    def reduce4(h, s):
        step = (1, 3)[s]
        value = line(h, step)
        net.wait(("r3", h, s), r3.at[h, s], far_dev(h, -step))
        for t in (0, 1):
            piece = value[32 * t : 32 * t + 32]
            if s == t:
                piece = piece + r3[h, s].astype(F32)
            st4[h, s, 32 * t : 32 * t + 32, :] = piece.astype(BF16)
        net.send(("r4", h, s), st4.at[h, s], r4.at[h, s], far_dev(h, step))

    def reduce5(h):
        value = line(h, 0)
        for s, step in enumerate((1, 3)):
            net.wait(("r4", h, s), r4.at[h, s], far_dev(h, -step))
        return value + r4[h, 0].astype(F32) + r4[h, 1].astype(F32)

    image_plan = {
        0: lambda: (reduce1(0, 2), reduce1(0, 1), reduce1(1, 2)),
        1: lambda: (reduce1(0, 3), reduce1(0, 0)),
        2: lambda: (reduce1(1, 1), reduce1(1, 3), reduce2(1, 2, 0), reduce2(1, 2, 1)),
        3: lambda: (reduce1(1, 0), reduce2(0, 2, 0), reduce2(0, 2, 1)),
        4: lambda: (reduce2(0, 1, 0), reduce2(0, 1, 1), reduce2(1, 1, 0), reduce2(1, 1, 1)),
        5: lambda: (reduce2(0, 3, 0), reduce2(0, 3, 1), reduce2(1, 3, 0), reduce2(1, 3, 1)),
        6: lambda: (reduce2(0, 0, 0), reduce2(0, 0, 1)),
        7: lambda: (reduce2(1, 0, 0), reduce2(1, 0, 1)),
    }

    def image_step(i, carry):
        at = pl.ds(pl.multiple_of(i * 256, 256), 256)
        total = jnp.dot(S[at, 0:1024], cols[0], preferred_element_type=F32)
        total = total + jnp.dot(S[at, 1024:2048], cols[1], preferred_element_type=F32)
        K[0, at, 0:D] = total
        for when, act in image_plan.items():
            @pl.when(i == when)
            def _(act=act):
                act()

        return carry

    lax.fori_loop(0, 8, image_step, 0)

    ORDER = (2, 1, 3, 0)

    def side_copy(m, k):
        return net.copy(("sib", m, k), gsib.at[m, k], sibgot.at[m, k], at_y(0, 0))

    def pair_sum(m, k):
        side_copy(m, k).wait_recv()
        at = (m * 4 + k) * B
        return K[1, at : at + B, 0:D] + sibgot[m, k].astype(F32)

    def ring1(m):
        yst1[m] = pair_sum(m, 0).astype(BF16)
        for s, step in enumerate((1, 3)):
            net.send(("y1", m, s), yst1.at[m, pl.ds(64 * s, 64), :], yr1.at[m, s], at_y(step))

    def ring2(m, s):
        step = (1, 3)[s]
        value = pair_sum(m, 1 + s)
        net.wait(("y1", m, s), yr1.at[m, s], at_y(-step))
        for t in (0, 1):
            piece = value[64 * t : 64 * t + 64]
            if s == t:
                piece = piece + yr1[m, s].astype(F32)
            yst2[m, s, 64 * t : 64 * t + 64, :] = piece.astype(BF16)
        net.send(("y2", m, s), yst2.at[m, s], yr2.at[m, s], at_y(step))

    def ring3(m):
        value = pair_sum(m, 3)
        for s, step in enumerate((1, 3)):
            net.wait(("y2", m, s), yr2.at[m, s], at_y(-step))
        return value + yr2[m, 0].astype(F32) + yr2[m, 1].astype(F32)

    column_plan = {
        1: lambda: (ring1(0), reduce3(0)),
        2: lambda: (ring1(1), reduce3(1)),
        4: lambda: (ring2(0, 0), reduce4(0, 0), reduce4(0, 1)),
        5: lambda: (ring2(1, 0), reduce4(1, 0), reduce4(1, 1)),
        6: lambda: (ring2(0, 1),),
        7: lambda: (ring2(1, 1),),
    }
    down = (((0,), (0,)), ((), ()))

    for k in range(4):
        for m in both:
            step = 2 * k + m
            total = lax.dot_general(
                S[:, m * 1024 + k * 256 : m * 1024 + k * 256 + 256], img[...], down, preferred_element_type=F32
            )
            gsib[m, k] = total[:B].astype(BF16)
            K[1, (m * 4 + k) * B : (m * 4 + k + 1) * B, 0:D] = total[B:]
            net.send(("sib", m, k), gsib.at[m, k], sibgot.at[m, k], at_y(0, 0))
            if step in column_plan:
                column_plan[step]()

    def finish(raw_ref, out_ref, rows, g):
        values = raw_ref[rows, :].astype(F32)
        inverse = lax.rsqrt(jnp.sum(values * values, axis=1, keepdims=True) + epsilon)
        unit = values * inverse
        g = g * (1.0 / logit_softness)
        out_ref[rows, :] = (g - unit * jnp.sum(unit * g, axis=1, keepdims=True)) * inverse

    for h in (0, 1):
        finish(img_in, out_img, slice(64 * h, 64 * h + 64), reduce5(h))
    finish(txt_in, out_txt, slice(0, B), ring3(0))
    finish(aud_in, out_aud, slice(0, B), ring3(1))

    net.drain()
    for m in both:
        for k in range(ITERS + 2):
            rows_whole(k, m).wait_send()
        for k in range(ITERS + 1):
            cols_whole(k, m).wait_send()


def shards(images, texts, audio):
    whole = pl.BlockSpec(memory_space=pltpu.VMEM)
    shape = jax.ShapeDtypeStruct(images.shape, F32)
    rounds_r, rounds_c = ITERS + 2, ITERS + 1
    return pl.pallas_call(
        kernel,
        out_shape=(shape, shape, shape),
        in_specs=[whole] * 3,
        out_specs=[whole] * 3,
        scratch_shapes=[
            pltpu.VMEM((2048, D), BF16),
            pltpu.VMEM((2, 1024, D), BF16),
            pltpu.VMEM((2, 2048, 1024), F32),
            pltpu.VMEM((2, 2048, 1024), F32),
            pltpu.VMEM((2048, 2048), BF16),
            pltpu.VMEM((2, 16, B), F32),
            pltpu.VMEM((rounds_r, 2, 16, B), F32),
            pltpu.VMEM((rounds_r, 2, 15, 16, B), F32),
            pltpu.VMEM((2, 8, B), F32),
            pltpu.VMEM((rounds_c, 2, 8, B), F32),
            pltpu.VMEM((rounds_c, 2, 7, 8, B), F32),
            pltpu.VMEM((2, 16, B), F32),
            pltpu.VMEM((2, 8, B), F32),
            pltpu.VMEM((2, 16, B), F32),
            pltpu.VMEM((2, 8, B), F32),
            pltpu.VMEM((2, 4, 64, D), BF16),
            pltpu.VMEM((2, 4, 2, 32, D), BF16),
            pltpu.VMEM((2, 4, 2, 64, D), BF16),
            pltpu.VMEM((2, 4, 2, 64, D), BF16),
            pltpu.VMEM((2, 64, D), BF16),
            pltpu.VMEM((2, 2, 32, D), BF16),
            pltpu.VMEM((2, 2, 64, D), BF16),
            pltpu.VMEM((2, 2, 64, D), BF16),
            pltpu.VMEM((2, 4, B, D), BF16),
            pltpu.VMEM((2, 4, B, D), BF16),
            pltpu.VMEM((2, B, D), BF16),
            pltpu.VMEM((2, 2, 64, D), BF16),
            pltpu.VMEM((2, 2, B, D), BF16),
            pltpu.VMEM((2, 2, B, D), BF16),
            pltpu.SemaphoreType.DMA((NSEM,)),
            pltpu.SemaphoreType.DMA((NSEM,)),
            pltpu.SemaphoreType.DMA((rounds_r, 2)),
            pltpu.SemaphoreType.DMA((rounds_r, 2)),
            pltpu.SemaphoreType.DMA((rounds_c, 2)),
            pltpu.SemaphoreType.DMA((rounds_c, 2)),
        ],
        compiler_params=pltpu.CompilerParams(
            collective_id=0, has_side_effects=True, vmem_limit_bytes=67043328
        ),
    )(images, texts, audio)


def solution(mesh):
    by_row = P(("row", "col"), None)
    by_col = P(("col", "row"), None)
    return jax.shard_map(
        shards,
        mesh=mesh,
        in_specs=(by_row, by_col, by_col),
        out_specs=(by_row, by_col, by_col),
        check_vma=False,
    )
```

time: 330 us -> 130 us (0.39)
  Pallas kernels: 0 us -> 125 us
  waiting for transfers between devices: 122 us -> 0 us
  other arithmetic: 75.1 us -> 0 us
  blocking collectives: 64.5 us -> 0 us
  matrix products: 32.5 us -> 0 us
  between operations: 14.1 us -> 0.65 us
  local copies, waits for them, and re-layouts: 13.1 us -> 3.7 us
  starting transfers between devices: 7.57 us -> 0 us
    pallas_call x0 -> x1, Pallas kernels: none -> 125 us  [shards(): pl.pallas_call(kernel, out_shape=(shape, shape, shape), in_specs=[whole]...]
    all_gather x2 -> x0, waiting for transfers between devices: 74.9 us -> none  [the longest x1 47.4 us: shards(): lax.all_gather(img_unit.astype(jnp.bfloat16), COL, axis=0, tiled=True)]
    all_to_all x6 -> x0, blocking collectives: 64.5 us -> none  [from_everyone(): lax.all_to_all(jnp.broadcast_to(value[None], (size, *value.shape)), axis,...]
    reduce_sum x19 -> x0, other arithmetic: 53.9 us -> none  [the longest x3 25.7 us: shards(): jnp.sum(loss_routine * rows_scale[:, :, None], axis=0)]
    dot_general x4 -> x0, matrix products: 32.5 us -> none  [the longest x1 14.3 us: shards(): lax.dot_general(img_rows, paired_cols, contract, preferred_element_type=j...]
    all_to_all x2 -> x0, waiting for transfers between devices: 27.7 us -> none  [the longest x1 20.6 us: summed_on_arrival(): lax.all_to_all(blocks, axis, split_axis=0, concat_axis=0, tiled=True)]
    reduce_scatter x2 -> x0, waiting for transfers between devices: 19.7 us -> none  [summed_rows(): subtotal = lax.psum_scatter(subtotal, axis, scatter_dimension=0, tiled=True)]
    convert_element_type x4 -> x0, other arithmetic: 17.3 us -> none  [the longest x1 12.1 us: shards(): score_grad.astype(jnp.bfloat16).reshape(row_extent, 2 * column_width)]
  transfers between devices with their start and end apart: 6 -> 0, of which waited for: 6 -> 0; matrix products, arithmetic and copies ran while one was open for 6% -> 0% of each run, Pallas kernels for 0% -> 0%
where the time goes in v1:
time: 130 us; the launch traced here: 129 us
  Pallas kernels  125 us (96%)
  local copies, waits for them, and re-layouts  3.7 us (3%)
    pallas_call x1, Pallas kernels, shards(): pl.pallas_call(kernel, out_shape=(shape, shape, shape), in_specs=[whole]...  125 us
    unnamed x7, local copies, waits for them, and re-layouts  3.7 us

profile of v1, /device:TPU:0, one launch (start us, length us, event | category | flops | bytes accessed | tf_op | source)
XLA Modules:
  0.0 129.4 jit_solution(16739121389424204757)
XLA Ops:
  0.6 125.1 %shard_map.58 = (f32[128,768]{1,0:T(8,128)}, f32[128,768]{1,0:T(8,128)}, f32[128,768]{1,0:T(8,128)}) custom-call(bf16[128,768]{1,0:T(8,128)(2,1)} %img_in.1, bf16[128,768]{1,0:T(8,128)(2,1)} %txt_in.1, bf16[128,768]{1,0:T(8,128)(2,1)} %aud_in.1), custom_call_target="tpu_custom_call" | custom-call | tf_op jit(solution)/shard_map/pallas_call | solution.py:515
  125.7 0.0 copy-start.1
  125.7 1.8 %copy.9 = f32[128,768]{1,0:T(8,128)} copy(f32[128,768]{1,0:T(8,128)} %get-tuple-element.6) | data formatting | bytes 786432
  127.5 0.0 copy-done.1
  127.6 0.0 copy-start
  127.6 0.7 copy.10
  128.3 0.4 copy-done
  128.7 0.7 copy.11
Async XLA Ops:
  125.7 1.8 %copy-start.1 = (f32[128,768]{1,0:T(8,128)S(1)}, f32[128,768]{1,0:T(8,128)}, u32[]{:S(2)}) copy-start(f32[128,768]{1,0:T(8,128)} %get-tuple-element.7) | copy-start | bytes 1179652
  127.6 1.1 copy-start
